TPU v7x, 32 devices: a whole 2x2x4 slice. The times are simulated.
32 devices in a mesh: dap: 32 (over z, y, x, core).
Axes of the slice: x: 2, y: 2, z: 4, core: 2. Of those that a mesh axis runs over, the one named last changes fastest.
Arguments:
- pair: bfloat16 [128, 128, 128], P('dap'), may hold values from -6 to 6
- residue_mask: int32 [128], P('dap'), may hold values 0 or 1
- norm_gain: float32 [2, 128], replicated, may hold values from 0.5 to 1.5
- proj_weight: bfloat16 [2, 128, 512], replicated, may hold values from -0.5 to 0.5
- gate_weight: bfloat16 [2, 128, 128], replicated, may hold values from -0.5 to 0.5
- mix_gain: float32 [2, 128], replicated, may hold values from 0.5 to 1.5
- out_weight: bfloat16 [2, 128, 128], replicated, may hold values from -0.5 to 0.5
Outputs:
- updated_pair: bfloat16 [128, 128, 128], P('dap')
All inputs are finite; a program needn't handle non-finite values. No bound on the sum of `residue_mask` on one device may be relied on, other than what follows from the above.
Results may differ from a plain program's by a relative error of at most 0.0061.
Values may be sent and summed in bfloat16 or wider, within the bound.
A program may use at most 64 MiB of HBM per device.

v0:
```python
import functools

import jax
import jax.numpy as jnp
from jax import lax
from jax.experimental import pallas as pl
from jax.experimental.pallas import tpu as pltpu
from jax.sharding import PartitionSpec as P

EPS = 1e-05
F32 = jnp.float32
BF16 = jnp.bfloat16
MESH = pl.DeviceIdType.MESH
HALVES = 2


def normalize(values, axis):
    center = values - jnp.mean(values, axis=axis, keepdims=True)
    spread = jnp.mean(center * center, axis=axis, keepdims=True)
    return center * lax.rsqrt(spread + EPS)


def dot(a, b, dims):
    return lax.dot_general(a, b, ((dims[:1], dims[1:]), ((), ())), preferred_element_type=F32)


def fused_kernel(
    devices,
    pair_hbm,
    mask_hbm,
    norm_hbm,
    proj_hbm,
    gate_hbm,
    mix_hbm,
    outw_hbm,
    out_ref,
    pair_ref,
    mask_ref,
    norm_ref,
    proj_ref,
    gate_ref,
    mix_ref,
    outw_ref,
    wide_send,
    wide_recv,
    cross_recv,
    tri_send,
    tri_recv,
    part_send,
    part_recv,
    mask_send,
    mask_recv,
    weight_s,
    gate_s,
    gain_s,
    state_s,
    stage_s,
    left_s,
    right_s,
    flat_s,
    part_s,
    square_s,
    send_sems,
    recv_sems,
    load_sems,
):
    sources = (pair_hbm, proj_hbm, mask_hbm, norm_hbm, gate_hbm, mix_hbm, outw_hbm)
    places = (pair_ref, proj_ref, mask_ref, norm_ref, gate_ref, mix_ref, outw_ref)
    loads = [
        pltpu.make_async_copy(source, place, load_sems.at[slot])
        for slot, (source, place) in enumerate(zip(sources, places))
    ]
    for load in loads:
        load.start()
    rows, total, chans = pair_ref.shape
    hidden = mix_ref.shape[1]
    group = devices // HALVES
    own = hidden // group
    me = lax.axis_index("dap")
    first = (me // group) * group
    spot = lax.rem(me, group)

    barrier = pltpu.get_barrier_semaphore()

    def greet(step, carry):
        peer = lax.rem(me + step, devices)
        pl.semaphore_signal(barrier, inc=1, device_id=(peer,), device_id_type=MESH)
        return carry

    lax.fori_loop(1, devices, greet, 0)

    def peer_of(step, size):
        if size != devices and size & (size - 1) == 0:
            return me ^ (size - step)
        base = (me // size) * size
        return base + lax.rem(me - base + step, size)

    def send_all(src, dst, size, slot):
        def one(step, carry):
            peer = peer_of(step, size)
            pltpu.make_async_remote_copy(
                src_ref=src(peer),
                dst_ref=dst,
                send_sem=send_sems.at[slot],
                recv_sem=recv_sems.at[slot],
                device_id=(peer,),
                device_id_type=MESH,
            ).start()
            return carry

        lax.fori_loop(1, size, one, 0)

    def wait_bytes(buf, count, sem):
        part = buf.at[pl.ds(0, count)]
        pltpu.make_async_copy(part, part, sem).wait()

    def turn_weights(layer):
        size = 4 * hidden
        i = lax.broadcasted_iota(jnp.int32, (size, size), 0)
        j = lax.broadcasted_iota(jnp.int32, (size, size), 1)
        pick = jnp.where(i == j, 1.0, 0.0).astype(BF16)
        weight_s[layer] = dot(pick, proj_ref[layer], (1, 1)).astype(BF16)

    def norm_of(layer):
        z = state_s[...].astype(F32)
        return (normalize(z, 1) * norm_ref[pl.ds(layer, 1), :]).astype(BF16)

    def make_panels(layer, normed, column_mask):
        for r in range(rows):
            scale = mask_ref[r].astype(F32)
            if column_mask is not None:
                scale = column_mask * scale
            part = normed[r * total : (r + 1) * total]
            for side in range(2):
                at = 2 * side * hidden
                gate = dot(weight_s[layer, at : at + hidden], part, (1, 1))
                value = dot(weight_s[layer, at + hidden : at + 2 * hidden], part, (1, 1))
                panel = jax.nn.sigmoid(gate) * value * scale
                wide_send[layer, side, :, r] = panel.reshape(group, own, total).astype(BF16)

    def make_gate(layer, normed):
        gate_s[...] = jax.nn.sigmoid(dot(normed, gate_ref[layer], (1, 0)))

    def unpack(panel, stage):
        for r in range(rows):
            stage[r] = panel[:, r].astype(F32).reshape(panel.shape[0] * own, total)

    def panel_of(stage, count, c):
        return [stage.at[r][pl.ds(c, count, stride=own), :] for r in range(rows)]

    def outgoing(mask_row):
        for c in range(own):
            for r, right in enumerate(panel_of(stage_s, devices, c)):
                square_s[c % 2, pl.ds(r, devices, stride=rows), :] = right
            left = jnp.concatenate(panel_of(left_s, group, c), axis=0)
            tri = dot((left * mask_row).astype(BF16), square_s[c % 2].astype(BF16), (1, 1))
            for r in range(rows):
                flat_s[pl.ds(c * rows + r, group, stride=own * rows), :] = tri[
                    r * group : (r + 1) * group
                ]
        tri_send[...] = flat_s[...].reshape(group, own * rows, total).astype(BF16)

    def incoming():
        for c in range(own):
            left = jnp.concatenate(panel_of(left_s, group, c), axis=0).astype(BF16)
            right = jnp.concatenate(panel_of(right_s, group, c), axis=0).astype(BF16)
            square_s[c % 2] = dot(left, right, (0, 0))
            for r in range(rows):
                part_s[pl.ds(c * rows + r, devices, stride=own * rows), :] = square_s[
                    c % 2, pl.ds(r, devices, stride=rows), :
                ]
        part_send[...] = part_s[...].reshape(devices, own * rows, total).astype(BF16)

    def finish(layer, products):
        flat_s[...] = products.reshape(hidden * rows, total)
        for r in range(rows):
            tri = flat_s[pl.ds(r, hidden, stride=rows), :]
            tri_normed = (normalize(tri, 0) * gain_s[layer]).astype(BF16)
            out = dot(tri_normed, outw_ref[layer], (0, 0))
            block = pl.ds(r * total, total)
            new = (state_s[block, :].astype(F32) + gate_s[block, :] * out).astype(BF16)
            if layer == 0:
                state_s[block, :] = new
            else:
                out_ref[r] = new

    for load in loads:
        load.wait()
    lane = lax.broadcasted_iota(jnp.int32, (1, total), 1)
    mask_row = jnp.zeros((1, total), F32)
    for r in range(rows):
        mask_row = mask_row + jnp.where(lane == me * rows + r, mask_ref[r].astype(F32), 0.0)
    mask_send[...] = mask_row
    state_s[...] = pair_ref[...].reshape(rows * total, chans)
    turn_weights(0)
    for layer in range(2):
        gain_s[layer] = jnp.broadcast_to(mix_ref[pl.ds(layer, 1), :], (total, hidden)).T
    normed = norm_of(0)
    make_panels(0, normed, None)
    pl.semaphore_wait(barrier, devices - 1)
    send_all(lambda peer: mask_send, mask_recv.at[me], devices, 0)
    send_all(
        lambda peer: wide_send.at[0, 1, lax.rem(peer, group)], cross_recv.at[me], devices, 1
    )
    send_all(
        lambda peer: wide_send.at[0, 0, lax.rem(peer, group)], wide_recv.at[0, spot], group, 2
    )
    mask_recv[me] = mask_send[...]
    cross_recv[me] = wide_send[0, 1, spot]
    wide_recv[0, spot] = wide_send[0, 0, spot]
    make_gate(0, normed)
    turn_weights(1)
    wait_bytes(mask_recv, devices - 1, recv_sems.at[0])
    column_mask = jnp.sum(mask_recv[...], axis=0)
    wait_bytes(wide_recv.at[0], group - 1, recv_sems.at[2])
    unpack(wide_recv[0], left_s)
    wait_bytes(cross_recv, devices - 1, recv_sems.at[1])
    unpack(cross_recv[...], stage_s)
    outgoing(column_mask)
    send_all(lambda peer: tri_send.at[peer - first], tri_recv.at[spot], group, 3)
    tri_recv[spot] = tri_send[spot]
    wait_bytes(tri_recv, group - 1, recv_sems.at[3])
    finish(0, tri_recv[...].astype(F32))
    normed = norm_of(1)
    make_panels(1, normed, column_mask)
    for side in range(2):
        send_all(
            lambda peer: wide_send.at[1, side, peer - first],
            wide_recv.at[1 + side, spot],
            group,
            4 + side,
        )
        wide_recv[1 + side, spot] = wide_send[1, side, spot]
    make_gate(1, normed)
    wait_bytes(wide_recv.at[1], group - 1, recv_sems.at[4])
    unpack(wide_recv[1], left_s)
    wait_bytes(wide_recv.at[2], group - 1, recv_sems.at[5])
    unpack(wide_recv[2], right_s)
    incoming()
    send_all(lambda peer: part_send.at[peer], part_recv.at[me], devices, 6)
    part_recv[me] = part_send[me]
    wait_bytes(mask_recv, devices - 1, send_sems.at[0])
    wait_bytes(cross_recv, devices - 1, send_sems.at[1])
    wait_bytes(wide_send.at[0, 0], group - 1, send_sems.at[2])
    wait_bytes(tri_send, group - 1, send_sems.at[3])
    wait_bytes(wide_send.at[1, 0], group - 1, send_sems.at[4])
    wait_bytes(wide_send.at[1, 1], group - 1, send_sems.at[5])
    wait_bytes(part_recv, devices - 1, recv_sems.at[6])
    products = part_recv[0:group].astype(F32)
    for half in range(1, HALVES):
        products = products + part_recv[half * group : (half + 1) * group].astype(F32)
    finish(1, products)
    wait_bytes(part_send, devices - 1, send_sems.at[6])


def fused(devices, pair, residue_mask, norm_gain, proj_weight, gate_weight, mix_gain, out_weight):
    rows, total, chans = pair.shape
    hidden = mix_gain.shape[1]
    group = devices // HALVES
    own = hidden // group
    hbm = pl.BlockSpec(memory_space=pltpu.HBM)
    params = (norm_gain, proj_weight, gate_weight, mix_gain, out_weight)
    return pl.pallas_call(
        functools.partial(fused_kernel, devices),
        out_shape=jax.ShapeDtypeStruct((rows, total, chans), BF16),
        in_specs=[hbm] * 7,
        out_specs=pl.BlockSpec(memory_space=pltpu.VMEM),
        scratch_shapes=[
            pltpu.VMEM(pair.shape, BF16),
            pltpu.SMEM(residue_mask.shape, jnp.int32),
            *(pltpu.VMEM(p.shape, p.dtype) for p in params),
            pltpu.VMEM((2, 2, group, rows, own, total), BF16),
            pltpu.VMEM((3, group, rows, own, total), BF16),
            pltpu.VMEM((devices, rows, own, total), BF16),
            pltpu.VMEM((group, own * rows, total), BF16),
            pltpu.VMEM((group, own * rows, total), BF16),
            pltpu.VMEM((devices, own * rows, total), BF16),
            pltpu.VMEM((devices, own * rows, total), BF16),
            pltpu.VMEM((1, total), F32),
            pltpu.VMEM((devices, 1, total), F32),
            pltpu.VMEM((2, 4 * hidden, chans), BF16),
            pltpu.VMEM((rows * total, chans), F32),
            pltpu.VMEM((2, hidden, total), F32),
            pltpu.VMEM((rows * total, chans), BF16),
            pltpu.VMEM((rows, devices * own, total), F32),
            pltpu.VMEM((rows, group * own, total), F32),
            pltpu.VMEM((rows, group * own, total), F32),
            pltpu.VMEM((hidden * rows, total), F32),
            pltpu.VMEM((devices * own * rows, total), F32),
            pltpu.VMEM((2, total, total), F32),
            pltpu.SemaphoreType.DMA((7,)),
            pltpu.SemaphoreType.DMA((7,)),
            pltpu.SemaphoreType.DMA((7,)),
        ],
        compiler_params=pltpu.CompilerParams(
            collective_id=0, has_side_effects=True, vmem_limit_bytes=67043328
        ),
        name="triangles",
    )(pair, residue_mask, *params)


def panels(rows, mask_rows, mask_all, gain, weight):
    hidden = weight.shape[1] // 4
    mask_float = mask_all.astype(F32)
    normed = (normalize(rows.astype(F32), 2) * gain).astype(BF16)
    proj = jnp.einsum("rnc,ch->hrn", normed, weight, preferred_element_type=F32)
    scale = mask_rows.astype(F32)[:, None] * mask_float[None, :]
    left = (jax.nn.sigmoid(proj[:hidden]) * proj[hidden : 2 * hidden] * scale).astype(BF16)
    right = (jax.nn.sigmoid(proj[2 * hidden : 3 * hidden]) * proj[3 * hidden :] * scale).astype(
        BF16
    )
    return (normed, left, right)


def triangle(rows, mask_rows, mask_all, gain, weight, gate_w, tri_gain, out_w, second):
    normed, left, right = panels(rows, mask_rows, mask_all, gain, weight)
    left = lax.all_to_all(left, "dap", split_axis=0, concat_axis=1, tiled=True)
    right = lax.all_to_all(right, "dap", split_axis=0, concat_axis=1, tiled=True)
    spec = "cki,ckj->cij" if second else "cik,cjk->cij"
    tri = jnp.einsum(spec, left, right, preferred_element_type=F32).astype(BF16)
    tri = lax.all_to_all(tri, "dap", split_axis=1, concat_axis=0, tiled=True)
    gate = jax.nn.sigmoid(jnp.einsum("rnc,cd->rnd", normed, gate_w, preferred_element_type=F32))
    tri_normed = (normalize(tri.astype(F32), 0) * tri_gain[:, None, None]).astype(BF16)
    out = jnp.einsum("hrn,hc->rnc", tri_normed, out_w, preferred_element_type=F32)
    return (rows.astype(F32) + gate * out).astype(BF16)


def by_collectives(pair, residue_mask, *params):
    mask_all = lax.all_gather(residue_mask, "dap", axis=0, tiled=True)
    state = pair
    for layer in range(2):
        gain, weight, gate_w, tri_gain, out_w = (p[layer] for p in params)
        state = triangle(
            state, residue_mask, mask_all, gain, weight, gate_w, tri_gain, out_w, layer == 1
        )
    return state


def solution(mesh):
    devices = mesh.shape["dap"]

    def body(pair, residue_mask, norm_gain, proj_weight, gate_weight, mix_gain, out_weight):
        args = (pair, residue_mask, norm_gain, proj_weight, gate_weight, mix_gain, out_weight)
        group = devices // HALVES
        own = mix_gain.shape[1] // group
        whole = group * HALVES == devices and own * group == mix_gain.shape[1]
        if whole and own % 8 == 0 and pair.shape[1] == 128:
            return fused(devices, *args)
        return by_collectives(*args)

    return jax.shard_map(
        body,
        mesh=mesh,
        in_specs=(P("dap", None, None), P("dap"), P(), P(), P(), P(), P()),
        out_specs=P("dap", None, None),
        check_vma=False,
    )
```

profile of v0, /device:TPU:0, one launch (start us, length us, event | category | flops | bytes accessed | tf_op | source)
XLA Modules:
  0.0 35.3 jit_solution(11306001985719951760)
XLA Ops:
  0.0 33.8 %triangles.1 = bf16[4,128,128]{2,1,0:T(8,128)(2,1)} custom-call(bf16[4,128,128]{2,1,0:T(8,128)(2,1)} %pair_hbm.1, s32[4]{0:T(128)} %mask_hbm.1, f32[2,128]{1,0:T(2,128)} %norm_hbm.1, bf16[2,128,512]{2,1,0:T(8,128)(2,1)} %proj_hbm.1, bf16[2,128,128]{2,1,0:T(8,128)(2,1)} %gate_hbm.1, f32[2,128]{1,0:T(2,128)} %mix_hbm.1, bf16[2,128,128]{2,1,0:T(8,128)(2,1)} %outw_hbm.1), custom_call_target="tpu_custom_call" | custom-call | tf_op jit(solution)/shard_map/triangles/pallas_call | solution.py:263
  33.8 1.6 %copy.9 = bf16[4,128,128]{2,1,0:T(8,128)(2,1)} copy(bf16[4,128,128]{2,1,0:T(8,128)(2,1)} %triangles.1) | data formatting | bytes 262144
where the time goes:
time: 35.5 us; the launch traced here: 35.3 us
  Pallas kernels  33.8 us (95%)
  local copies, waits for them, and re-layouts  1.57 us (4%)
    pallas_call x1, Pallas kernels, fused(): pl.pallas_call(functools.partial(fused_kernel, devices), out_shape=jax.Sh...  33.8 us
    unnamed x1, local copies, waits for them, and re-layouts  1.57 us

commit v1 on v0

--- a/solution.py
+++ b/solution.py
@@ -262,7 +262,7 @@
     params = (norm_gain, proj_weight, gate_weight, mix_gain, out_weight)
     return pl.pallas_call(
         functools.partial(fused_kernel, devices),
-        out_shape=jax.ShapeDtypeStruct((rows, total, chans), BF16),
+        out_shape=pltpu.VMEM((rows, total, chans), BF16),
         in_specs=[hbm] * 7,
         out_specs=pl.BlockSpec(memory_space=pltpu.VMEM),
         scratch_shapes=[
@@ -293,10 +293,10 @@
             pltpu.SemaphoreType.DMA((7,)),
         ],
         compiler_params=pltpu.CompilerParams(
-            collective_id=0, has_side_effects=True, vmem_limit_bytes=67043328
+            collective_id=0, has_side_effects=True, vmem_limit_bytes=16777216
         ),
         name="triangles",
-    )(pair, residue_mask, *params)
+    )(*(pltpu.with_memory_space_constraint(v, pltpu.HBM) for v in (pair, residue_mask, *params)))
 
 
 def panels(rows, mask_rows, mask_all, gain, weight):

time: 35.5 us -> 33.9 us (0.955)
  local copies, waits for them, and re-layouts: 1.57 us -> 0.66 us
  Pallas kernels: 33.8 us -> 33.1 us
    unnamed x1, local copies, waits for them, and re-layouts: 1.57 us -> 0.66 us
    pallas_call x1, Pallas kernels: 33.8 us -> 33.1 us  [fused(): pl.pallas_call(functools.partial(fused_kernel, devices), out_shape=pltpu....]
where the time goes in v1:
time: 33.9 us; the launch traced here: 33.8 us
  Pallas kernels  33.1 us (98%)
  local copies, waits for them, and re-layouts  0.66 us (2%)
    pallas_call x1, Pallas kernels, fused(): pl.pallas_call(functools.partial(fused_kernel, devices), out_shape=pltpu....  33.1 us

profile of v1, /device:TPU:0, one launch (start us, length us, event | category | flops | bytes accessed | tf_op | source)
XLA Modules:
  0.0 33.8 jit_solution(7570067389820224749)
XLA Ops:
  0.0 33.1 %triangles.1 = bf16[4,128,128]{2,1,0:T(8,128)(2,1)S(1)} custom-call(bf16[4,128,128]{2,1,0:T(8,128)(2,1)} %pair_hbm.1, s32[4]{0:T(128)} %mask_hbm.1, f32[2,128]{1,0:T(2,128)} %norm_hbm.1, bf16[2,128,512]{2,1,0:T(8,128)(2,1)} %proj_hbm.1, bf16[2,128,128]{2,1,0:T(8,128)(2,1)} %gate_hbm.1, f32[2,128]{1,0:T(2,128)} %mix_hbm.1, bf16[2,128,128]{2,1,0:T(8,128)(2,1)} %outw_hbm.1), custom_call_target="tpu_custom_call" | custom-call | tf_op jit(solution)/shard_map/triangles/pallas_call | solution.py:263
  33.1 0.7 %copy.9 = bf16[4,128,128]{2,1,0:T(8,128)(2,1)} copy(bf16[4,128,128]{2,1,0:T(8,128)(2,1)S(1)} %triangles.1) | data formatting | bytes 262144

commit v2 on v1

v2 whole, which is shorter than its diff:
```python
import contextlib
import functools

import jax
import jax.numpy as jnp
from jax import lax
from jax.experimental import pallas as pl
from jax.experimental.pallas import tpu as pltpu
from jax.sharding import PartitionSpec as P

EPS = 1e-05
F32 = jnp.float32
BF16 = jnp.bfloat16
MESH = pl.DeviceIdType.MESH
HALVES = 2


def normalize(values, axis):
    center = values - jnp.mean(values, axis=axis, keepdims=True)
    spread = jnp.mean(center * center, axis=axis, keepdims=True)
    return center * lax.rsqrt(spread + EPS)


def dot(a, b, dims):
    return lax.dot_general(a, b, ((dims[:1], dims[1:]), ((), ())), preferred_element_type=F32)


def mark(name):
    return contextlib.nullcontext()


def fused_kernel(
    devices,
    pair_hbm,
    mask_hbm,
    norm_hbm,
    proj_hbm,
    gate_hbm,
    mix_hbm,
    outw_hbm,
    out_ref,
    pair_ref,
    mask_ref,
    norm_ref,
    proj_ref,
    gate_ref,
    mix_ref,
    outw_ref,
    mask_send,
    mask_recv,
    a_send,
    a_near,
    a_far,
    pair_far,
    b_send,
    b_recv,
    c_send,
    c_near,
    c_far,
    back_recv,
    d_send,
    d_recv,
    weight_s,
    gatew_s,
    outw_s,
    mixg_s,
    normg_s,
    scale_s,
    normed_s,
    normed1_s,
    zt_s,
    z1t_s,
    gate0_s,
    z1_s,
    gate1_s,
    left_s,
    right_s,
    rhs_s,
    flat_s,
    lhs1_s,
    own1_s,
    far1_s,
    flat1_s,
    send_sems,
    recv_sems,
    load_sems,
):
    sources = (pair_hbm, proj_hbm, mask_hbm, norm_hbm, gate_hbm, mix_hbm, outw_hbm)
    places = (pair_ref, proj_ref, mask_ref, norm_ref, gate_ref, mix_ref, outw_ref)
    loads = [
        pltpu.make_async_copy(source, place, load_sems.at[slot])
        for slot, (source, place) in enumerate(zip(sources, places))
    ]
    for load in loads:
        load.start()
    rows, total, chans = pair_ref.shape
    hidden = mix_ref.shape[1]
    group = devices // HALVES
    own = hidden // group
    cols = total // HALVES
    spots = rows * cols
    pairs = rows // 2
    me = lax.axis_index("dap")
    half = me // group
    spot = lax.rem(me, group)
    partner = lax.rem(me + group, devices)
    near_cols = pl.ds(pl.multiple_of(half * cols, cols), cols)
    far_cols = pl.ds(pl.multiple_of((1 - half) * cols, cols), cols)

    barrier = pltpu.get_barrier_semaphore()

    def greet(step, carry):
        peer = me ^ (devices - step)
        pl.semaphore_signal(barrier, inc=1, device_id=(peer,), device_id_type=MESH)
        return carry

    lax.fori_loop(1, devices, greet, 0)

    def push(src, dst, slot, peer):
        pltpu.make_async_remote_copy(
            src_ref=src,
            dst_ref=dst,
            send_sem=send_sems.at[slot],
            recv_sem=recv_sems.at[slot],
            device_id=(peer,),
            device_id_type=MESH,
        ).start()

    def push_near(src, dst, slot):
        def one(step, carry):
            bits = group - step
            push(src(spot ^ bits), dst, slot, me ^ bits)
            return carry

        lax.fori_loop(1, group, one, 0)

    def push_far(src, dst, slot):
        def one(step, carry):
            bits = group - step
            push(src(spot ^ bits), dst, slot, me ^ (group + bits))
            return carry

        lax.fori_loop(1, group + 1, one, 0)

    def push_all(src, dst, slot):
        def one(step, carry):
            push(src, dst, slot, me ^ (devices - step))
            return carry

        lax.fori_loop(1, devices, one, 0)

    def wait_all(buf, sem):
        pltpu.make_async_copy(buf, buf, sem).wait()

    def wait_some(buf, count, sem):
        part = buf.at[pl.ds(0, count)]
        pltpu.make_async_copy(part, part, sem).wait()

    def lanes_of(parts):
        return jnp.concatenate(parts, axis=1)

    def panels_of(layer, normed, dims, side):
        at = 2 * side * hidden
        gate = dot(weight_s[layer, at : at + hidden], normed, dims)
        value = dot(weight_s[layer, at + hidden : at + 2 * hidden], normed, dims)
        return jax.nn.sigmoid(gate) * value

    def make_panels0():
        for pair in range(pairs):
            normed = normed_s[2 * pair : 2 * pair + 2].reshape(2 * total, chans)
            for side in range(2):
                panel = panels_of(0, normed, (1, 1), side)
                parts = [
                    (panel[:, r * total : (r + 1) * total] * mask_ref[2 * pair + r].astype(F32))
                    for r in range(2)
                ]
                tile = jnp.concatenate([p.reshape(group, own, total) for p in parts], axis=1)
                at = pl.ds(2 * own * pair, 2 * own)
                a_send[:, side, at, :] = tile.astype(BF16)

    def make_gate0(part, normed):
        gate0_s[part] = jax.nn.sigmoid(dot(gatew_s[...], normed, (1, 1)))

    def turn(values):
        return values.astype(F32).T.astype(BF16)

    def set_scale(part, owner, column_mask, doubled):
        entry = [
            jnp.sum(jnp.where(lane == owner * rows + r, column_mask, 0.0), axis=1, keepdims=True)
            for r in range(rows)
        ]
        scale_s[part] = lanes_of(
            [
                jnp.where(lane < cols, entry[2 * p], entry[2 * p + 1]) * doubled
                for p in range(pairs)
            ]
        )

    def outgoing(part, panel):
        left_s[part] = panel.astype(F32).reshape(group * rows * own, total)
        for c in range(own):
            left = jnp.concatenate(
                [
                    lanes_of(
                        [
                            left_s[part, pl.ds((2 * p + r) * own + c, group, stride=rows * own), :]
                            for r in range(2)
                        ]
                    )
                    for p in range(pairs)
                ],
                axis=0,
            ).astype(BF16)
            tri = dot(left, rhs_s[c], (1, 1))
            for p in range(pairs):
                flat_s[part, pl.ds(p * own + c, group, stride=pairs * own), :] = tri[
                    p * group : (p + 1) * group
                ]
        b_send[part] = flat_s[part].reshape(group, pairs * own, total).astype(BF16)

    def send_b(part):
        push_near(lambda at: b_send.at[part, at], b_recv.at[part, spot], 5 + part)
        b_recv[part, spot] = b_send[part, spot]

    def finish0(part):
        got = b_recv[part].astype(F32)
        tri = lanes_of(
            [got[:, p * own : (p + 1) * own].reshape(hidden, total) for p in range(pairs)]
        )
        gain = mixg_s[0]
        tri_normed = (normalize(tri, 0) * lanes_of([gain] * pairs)).astype(BF16)
        out = dot(outw_s[...], tri_normed, (1, 0))
        new = (zt_s[part].astype(F32) + gate0_s[part] * out).astype(BF16)
        z1t_s[part] = new
        normed = (normalize(new.astype(F32), 0) * lanes_of([normg_s[...]] * pairs)).astype(BF16)
        if part == 0:
            normed1_s[...] = normed
        for side in range(2):
            panel = panels_of(1, normed, (1, 0), side) * scale_s[part]
            tile = jnp.concatenate(
                [
                    panel[:, p * total : (p + 1) * total].reshape(group, own, total)
                    for p in range(pairs)
                ],
                axis=1,
            )
            c_send[part, :, side] = tile.astype(BF16)

    def send_c(part):
        push_far(lambda at: c_send.at[part, at, 1], c_far.at[part, spot], 9 + part)
        push_near(lambda at: c_send.at[part, at], c_near.at[part, spot], 7 + part)
        c_near[part, spot] = c_send[part, spot]

    def natural(part, normed):
        gate1_s[part] = jax.nn.sigmoid(dot(normed, gate_ref[1], (1, 0)))

    def unpack1(part):
        size = group * pairs * own
        at = pl.ds(part * size, size)
        near = c_near[part].astype(F32)
        lhs1_s[at, :] = near[:, 0].reshape(size, total)
        own1_s[at, :] = near[:, 1].reshape(size, total)
        far1_s[at, :] = c_far[1 - part].astype(F32).reshape(size, total)

    def incoming():
        count = HALVES * group * pairs
        low = lane < cols
        for c in range(own):
            pick = pl.ds(c, count, stride=own)
            left = lhs1_s[pick, :].astype(BF16)
            right = lanes_of([own1_s[pick, :], far1_s[pick, :]]).astype(BF16)
            prod = dot(left, right, (0, 0))
            straight = jnp.where(low, prod[:cols, :total], prod[cols:, total:])
            crossed = jnp.where(low, prod[:cols, total:], prod[cols:, :total])
            tri = straight + pltpu.roll(crossed, cols, 1)
            flat1_s[pl.ds(c, cols, stride=own), :] = tri
        d_send[...] = flat1_s[...].reshape(group, rows * own, total).astype(BF16)

    def finish1():
        got = d_recv[...].astype(F32)
        for r in range(rows):
            tri = got[:, r * own : (r + 1) * own].reshape(hidden, total)
            tri_normed = (normalize(tri, 0) * mixg_s[1]).astype(BF16)
            out = dot(tri_normed, outw_ref[1], (0, 0))
            block = pl.ds(r * cols, cols)
            for part, place in enumerate((near_cols, far_cols)):
                piece = out[part * cols : (part + 1) * cols]
                new = z1_s[part, block, :].astype(F32) + gate1_s[part, block, :] * piece
                out_ref[r, place, :] = new.astype(BF16)

    lane = lax.broadcasted_iota(jnp.int32, (1, total), 1)
    with mark("load"):
        for load in loads:
            load.wait()
    with mark("panels0"):
        mask_row = jnp.zeros((1, total), F32)
        for r in range(rows):
            mask_row = mask_row + jnp.where(lane == me * rows + r, mask_ref[r].astype(F32), 0.0)
        mask_send[...] = mask_row
        weight_s[0] = turn(proj_ref[0])
        z = pair_ref[...].reshape(rows * total, chans).astype(F32)
        normed = (normalize(z, 1) * norm_ref[pl.ds(0, 1), :]).astype(BF16)
        normed_s[...] = normed.reshape(rows, total, chans)
        make_panels0()
    with mark("barrier"):
        pl.semaphore_wait(barrier, devices - 1)
    with mark("sendA"):
        push_all(mask_send, mask_recv.at[me], 0)
        push_far(lambda at: a_send.at[at, 0], a_far.at[spot], 2)
        push_near(lambda at: a_send.at[at], a_near.at[spot], 1)
        push(pair_ref.at[:, far_cols, :], pair_far, 3, partner)
        mask_recv[me] = mask_send[...]
        a_near[spot] = a_send[spot]
    with mark("idleA"):
        gatew_s[...] = turn(gate_ref[0])
        outw_s[...] = turn(outw_ref[0])
        weight_s[1] = turn(proj_ref[1])
        for layer in range(2):
            mixg_s[layer] = jnp.broadcast_to(mix_ref[pl.ds(layer, 1), :], (total, hidden)).T
        normg_s[...] = jnp.broadcast_to(norm_ref[pl.ds(1, 1), :], (total, chans)).T
        rhs_s[...] = jnp.zeros(rhs_s.shape, BF16)
        zt_s[0] = turn(pair_ref[:, near_cols, :].reshape(spots, chans))
        make_gate0(0, normed_s[:, near_cols, :].reshape(spots, chans))
    with mark("waitmask"):
        wait_some(mask_recv, devices - 1, recv_sems.at[0])
    with mark("masks"):
        column_mask = jnp.sum(mask_recv[...], axis=0)
        doubled = jnp.where(lane // cols == half, column_mask, pltpu.roll(column_mask, cols, 1))
        set_scale(0, me, column_mask, doubled)
        set_scale(1, partner, column_mask, doubled)
    with mark("waitAnear"):
        wait_some(a_near, group - 1, recv_sems.at[1])
    with mark("out0"):
        right_s[...] = a_near[:, 1].astype(F32).reshape(group * rows * own, total)
        for c in range(own):
            right = (right_s[pl.ds(c, cols, stride=own), :] * column_mask).astype(BF16)
            rhs_s[c, 0:cols, 0:total] = right
            rhs_s[c, cols : 2 * cols, total : 2 * total] = right
        outgoing(0, a_near[:, 0])
    with mark("sendB0"):
        send_b(0)
    with mark("waitAfar"):
        wait_all(a_far, recv_sems.at[2])
    with mark("out1"):
        outgoing(1, a_far[...])
    with mark("sendB1"):
        send_b(1)
    with mark("waitB0"):
        wait_some(b_recv.at[0], group - 1, recv_sems.at[5])
    with mark("fin0"):
        finish0(0)
    with mark("sendC0"):
        send_c(0)
    with mark("waitpair"):
        wait_all(pair_far, recv_sems.at[3])
    with mark("pair"):
        z = pair_far[...].reshape(spots, chans)
        zt_s[1] = turn(z)
        make_gate0(1, (normalize(z.astype(F32), 1) * norm_ref[pl.ds(0, 1), :]).astype(BF16))
    with mark("waitB1"):
        wait_some(b_recv.at[1], group - 1, recv_sems.at[6])
    with mark("fin1"):
        finish0(1)
    with mark("sendC1"):
        send_c(1)
        push(z1t_s.at[1], back_recv, 4, partner)
    with mark("nat0"):
        z1_s[0] = z1t_s[0].astype(F32).T.astype(BF16)
        natural(0, normed1_s[...].astype(F32).T.astype(BF16))
    with mark("waitC0"):
        wait_some(c_near.at[0], group - 1, recv_sems.at[7])
        wait_all(c_far.at[0], recv_sems.at[9])
    with mark("waitC1"):
        wait_some(c_near.at[1], group - 1, recv_sems.at[8])
        wait_all(c_far.at[1], recv_sems.at[10])
    with mark("in"):
        unpack1(0)
        unpack1(1)
        incoming()
    with mark("sendD"):
        push_near(lambda at: d_send.at[at], d_recv.at[spot], 11)
        d_recv[spot] = d_send[spot]
    with mark("waitback"):
        wait_all(back_recv, recv_sems.at[4])
    with mark("nat1"):
        z = back_recv[...].astype(F32).T
        z1_s[1] = z.astype(BF16)
        natural(1, (normalize(z, 1) * norm_ref[pl.ds(1, 1), :]).astype(BF16))
        wait_some(mask_recv, devices - 1, send_sems.at[0])
        wait_some(a_near, group - 1, send_sems.at[1])
        wait_all(a_far, send_sems.at[2])
        wait_all(pair_far, send_sems.at[3])
        wait_all(back_recv, send_sems.at[4])
        for part in range(2):
            wait_some(b_recv.at[part], group - 1, send_sems.at[5 + part])
            wait_some(c_near.at[part], group - 1, send_sems.at[7 + part])
            wait_all(c_far.at[part], send_sems.at[9 + part])
    with mark("waitD"):
        wait_some(d_recv, group - 1, recv_sems.at[11])
    with mark("finish1"):
        finish1()
    wait_some(d_recv, group - 1, send_sems.at[11])


def fused(devices, pair, residue_mask, norm_gain, proj_weight, gate_weight, mix_gain, out_weight):
    rows, total, chans = pair.shape
    hidden = mix_gain.shape[1]
    group = devices // HALVES
    own = hidden // group
    cols = total // HALVES
    spots = rows * cols
    pairs = rows // 2
    half_rows = group * pairs * own
    hbm = pl.BlockSpec(memory_space=pltpu.HBM)
    params = (norm_gain, proj_weight, gate_weight, mix_gain, out_weight)
    operands = [
        pltpu.with_memory_space_constraint(v, pltpu.HBM) for v in (pair, residue_mask, *params)
    ]
    return pl.pallas_call(
        functools.partial(fused_kernel, devices),
        out_shape=pltpu.VMEM(pair.shape, BF16),
        in_specs=[hbm] * 7,
        out_specs=pl.BlockSpec(memory_space=pltpu.VMEM),
        scratch_shapes=[
            pltpu.VMEM(pair.shape, BF16),
            pltpu.SMEM(residue_mask.shape, jnp.int32),
            *(pltpu.VMEM(p.shape, p.dtype) for p in params),
            pltpu.VMEM((1, total), F32),
            pltpu.VMEM((devices, 1, total), F32),
            pltpu.VMEM((group, 2, rows * own, total), BF16),
            pltpu.VMEM((group, 2, rows * own, total), BF16),
            pltpu.VMEM((group, rows * own, total), BF16),
            pltpu.VMEM((rows, cols, chans), BF16),
            pltpu.VMEM((2, group, pairs * own, total), BF16),
            pltpu.VMEM((2, group, pairs * own, total), BF16),
            pltpu.VMEM((2, group, 2, pairs * own, total), BF16),
            pltpu.VMEM((2, group, 2, pairs * own, total), BF16),
            pltpu.VMEM((2, group, pairs * own, total), BF16),
            pltpu.VMEM((chans, spots), BF16),
            pltpu.VMEM((group, rows * own, total), BF16),
            pltpu.VMEM((group, rows * own, total), BF16),
            pltpu.VMEM((2, 4 * hidden, chans), BF16),
            pltpu.VMEM((chans, chans), BF16),
            pltpu.VMEM((chans, hidden), BF16),
            pltpu.VMEM((2, hidden, total), F32),
            pltpu.VMEM((chans, total), F32),
            pltpu.VMEM((2, 1, spots), F32),
            pltpu.VMEM((rows, total, chans), BF16),
            pltpu.VMEM((chans, spots), BF16),
            pltpu.VMEM((2, chans, spots), BF16),
            pltpu.VMEM((2, chans, spots), BF16),
            pltpu.VMEM((2, chans, spots), F32),
            pltpu.VMEM((2, spots, chans), BF16),
            pltpu.VMEM((2, spots, chans), F32),
            pltpu.VMEM((2, group * rows * own, total), F32),
            pltpu.VMEM((group * rows * own, total), F32),
            pltpu.VMEM((own, total, 2 * total), BF16),
            pltpu.VMEM((2, half_rows, total), F32),
            pltpu.VMEM((2 * half_rows, total), F32),
            pltpu.VMEM((2 * half_rows, total), F32),
            pltpu.VMEM((2 * half_rows, total), F32),
            pltpu.VMEM((cols * own, total), F32),
            pltpu.SemaphoreType.DMA((12,)),
            pltpu.SemaphoreType.DMA((12,)),
            pltpu.SemaphoreType.DMA((7,)),
        ],
        compiler_params=pltpu.CompilerParams(
            collective_id=0, has_side_effects=True, vmem_limit_bytes=16777216
        ),
        name="triangles",
    )(*operands)


def panels(rows, mask_rows, mask_all, gain, weight):
    hidden = weight.shape[1] // 4
    mask_float = mask_all.astype(F32)
    normed = (normalize(rows.astype(F32), 2) * gain).astype(BF16)
    proj = jnp.einsum("rnc,ch->hrn", normed, weight, preferred_element_type=F32)
    scale = mask_rows.astype(F32)[:, None] * mask_float[None, :]
    left = (jax.nn.sigmoid(proj[:hidden]) * proj[hidden : 2 * hidden] * scale).astype(BF16)
    right = (jax.nn.sigmoid(proj[2 * hidden : 3 * hidden]) * proj[3 * hidden :] * scale).astype(
        BF16
    )
    return (normed, left, right)


def triangle(rows, mask_rows, mask_all, gain, weight, gate_w, tri_gain, out_w, second):
    normed, left, right = panels(rows, mask_rows, mask_all, gain, weight)
    left = lax.all_to_all(left, "dap", split_axis=0, concat_axis=1, tiled=True)
    right = lax.all_to_all(right, "dap", split_axis=0, concat_axis=1, tiled=True)
    spec = "cki,ckj->cij" if second else "cik,cjk->cij"
    tri = jnp.einsum(spec, left, right, preferred_element_type=F32).astype(BF16)
    tri = lax.all_to_all(tri, "dap", split_axis=1, concat_axis=0, tiled=True)
    gate = jax.nn.sigmoid(jnp.einsum("rnc,cd->rnd", normed, gate_w, preferred_element_type=F32))
    tri_normed = (normalize(tri.astype(F32), 0) * tri_gain[:, None, None]).astype(BF16)
    out = jnp.einsum("hrn,hc->rnc", tri_normed, out_w, preferred_element_type=F32)
    return (rows.astype(F32) + gate * out).astype(BF16)


def by_collectives(pair, residue_mask, *params):
    mask_all = lax.all_gather(residue_mask, "dap", axis=0, tiled=True)
    state = pair
    for layer in range(2):
        gain, weight, gate_w, tri_gain, out_w = (p[layer] for p in params)
        state = triangle(
            state, residue_mask, mask_all, gain, weight, gate_w, tri_gain, out_w, layer == 1
        )
    return state


def solution(mesh):
    devices = mesh.shape["dap"]

    def body(pair, residue_mask, norm_gain, proj_weight, gate_weight, mix_gain, out_weight):
        args = (pair, residue_mask, norm_gain, proj_weight, gate_weight, mix_gain, out_weight)
        group = devices // HALVES
        own = mix_gain.shape[1] // group
        rows, total, chans = pair.shape
        whole = group * HALVES == devices and group & (group - 1) == 0
        whole = whole and own * group == chans == mix_gain.shape[1] == total == 128
        if whole and own == 8 and rows == 4:
            return fused(devices, *args)
        return by_collectives(*args)

    return jax.shard_map(
        body,
        mesh=mesh,
        in_specs=(P("dap", None, None), P("dap"), P(), P(), P(), P(), P()),
        out_specs=P("dap", None, None),
        check_vma=False,
    )
```

time: 33.9 us -> 33.4 us (0.985)
  Pallas kernels: 33.1 us -> 32.6 us
    pallas_call x1, Pallas kernels: 33.1 us -> 32.6 us  [fused(): pl.pallas_call(functools.partial(fused_kernel, devices), out_shape=pltpu....]
where the time goes in v2:
time: 33.4 us; the launch traced here: 33.3 us
  Pallas kernels  32.6 us (98%)
  local copies, waits for them, and re-layouts  0.66 us (2%)
    pallas_call x1, Pallas kernels, fused(): pl.pallas_call(functools.partial(fused_kernel, devices), out_shape=pltpu....  32.6 us

profile of v2, /device:TPU:0, one launch (start us, length us, event | category | flops | bytes accessed | tf_op | source)
XLA Modules:
  0.0 33.3 jit_solution(14935483920435017165)
XLA Ops:
  0.0 32.6 %triangles.1 = bf16[4,128,128]{2,1,0:T(8,128)(2,1)S(1)} custom-call(bf16[4,128,128]{2,1,0:T(8,128)(2,1)} %pair_hbm.1, s32[4]{0:T(128)} %mask_hbm.1, f32[2,128]{1,0:T(2,128)} %norm_hbm.1, bf16[2,128,512]{2,1,0:T(8,128)(2,1)} %proj_hbm.1, bf16[2,128,128]{2,1,0:T(8,128)(2,1)} %gate_hbm.1, f32[2,128]{1,0:T(2,128)} %mix_hbm.1, bf16[2,128,128]{2,1,0:T(8,128)(2,1)} %outw_hbm.1), custom_call_target="tpu_custom_call" | custom-call | tf_op jit(solution)/shard_map/triangles/pallas_call | solution.py:419
  32.6 0.7 %copy.9 = bf16[4,128,128]{2,1,0:T(8,128)(2,1)} copy(bf16[4,128,128]{2,1,0:T(8,128)(2,1)S(1)} %triangles.1) | data formatting | bytes 262144

commit v3 on v2

--- a/solution.py
+++ b/solution.py
@@ -104,6 +104,8 @@
     half = me // group
     spot = lax.rem(me, group)
     partner = lax.rem(me + group, devices)
+    zone = me * 4 // devices
+    flip = jnp.where((zone == 0) | (zone == 3), group // 2, 0)
     near_cols = pl.ds(pl.multiple_of(half * cols, cols), cols)
     far_cols = pl.ds(pl.multiple_of((1 - half) * cols, cols), cols)
 
@@ -136,7 +138,7 @@
 
     def push_far(src, dst, slot):
         def one(step, carry):
-            bits = group - step
+            bits = (group - step) ^ flip
             push(src(spot ^ bits), dst, slot, me ^ (group + bits))
             return carry
 
@@ -306,9 +308,8 @@
         pl.semaphore_wait(barrier, devices - 1)
     with mark("sendA"):
         push_all(mask_send, mask_recv.at[me], 0)
+        push_near(lambda at: a_send.at[at], a_near.at[spot], 1)
         push_far(lambda at: a_send.at[at, 0], a_far.at[spot], 2)
-        push_near(lambda at: a_send.at[at], a_near.at[spot], 1)
-        push(pair_ref.at[:, far_cols, :], pair_far, 3, partner)
         mask_recv[me] = mask_send[...]
         a_near[spot] = a_send[spot]
     with mark("idleA"):
@@ -339,6 +340,7 @@
         outgoing(0, a_near[:, 0])
     with mark("sendB0"):
         send_b(0)
+        push(pair_ref.at[:, far_cols, :], pair_far, 3, partner)
     with mark("waitAfar"):
         wait_all(a_far, recv_sems.at[2])
     with mark("out1"):
@@ -363,10 +365,12 @@
         finish0(1)
     with mark("sendC1"):
         send_c(1)
-        push(z1t_s.at[1], back_recv, 4, partner)
     with mark("nat0"):
         z1_s[0] = z1t_s[0].astype(F32).T.astype(BF16)
         natural(0, normed1_s[...].astype(F32).T.astype(BF16))
+    with mark("back"):
+        wait_all(c_far.at[1], send_sems.at[10])
+        push(z1t_s.at[1], back_recv, 4, partner)
     with mark("waitC0"):
         wait_some(c_near.at[0], group - 1, recv_sems.at[7])
         wait_all(c_far.at[0], recv_sems.at[9])
@@ -391,10 +395,10 @@
         wait_all(a_far, send_sems.at[2])
         wait_all(pair_far, send_sems.at[3])
         wait_all(back_recv, send_sems.at[4])
+        wait_all(c_far.at[0], send_sems.at[9])
         for part in range(2):
             wait_some(b_recv.at[part], group - 1, send_sems.at[5 + part])
             wait_some(c_near.at[part], group - 1, send_sems.at[7 + part])
-            wait_all(c_far.at[part], send_sems.at[9 + part])
     with mark("waitD"):
         wait_some(d_recv, group - 1, recv_sems.at[11])
     with mark("finish1"):

time: 33.4 us -> 32 us (0.958)
  Pallas kernels: 32.6 us -> 31.2 us
    pallas_call x1, Pallas kernels: 32.6 us -> 31.2 us  [fused(): pl.pallas_call(functools.partial(fused_kernel, devices), out_shape=pltpu....]
where the time goes in v3:
time: 32 us; the launch traced here: 31.9 us
  Pallas kernels  31.2 us (98%)
  local copies, waits for them, and re-layouts  0.66 us (2%)
    pallas_call x1, Pallas kernels, fused(): pl.pallas_call(functools.partial(fused_kernel, devices), out_shape=pltpu....  31.2 us
    unnamed x1, local copies, waits for them, and re-layouts  0.66 us

profile of v3, /device:TPU:0, one launch (start us, length us, event | category | flops | bytes accessed | tf_op | source)
XLA Modules:
  0.0 31.9 jit_solution(9380509108103021627)
XLA Ops:
  0.0 31.2 %triangles.1 = bf16[4,128,128]{2,1,0:T(8,128)(2,1)S(1)} custom-call(bf16[4,128,128]{2,1,0:T(8,128)(2,1)} %pair_hbm.1, s32[4]{0:T(128)} %mask_hbm.1, f32[2,128]{1,0:T(2,128)} %norm_hbm.1, bf16[2,128,512]{2,1,0:T(8,128)(2,1)} %proj_hbm.1, bf16[2,128,128]{2,1,0:T(8,128)(2,1)} %gate_hbm.1, f32[2,128]{1,0:T(2,128)} %mix_hbm.1, bf16[2,128,128]{2,1,0:T(8,128)(2,1)} %outw_hbm.1), custom_call_target="tpu_custom_call" | custom-call | tf_op jit(solution)/shard_map/triangles/pallas_call | solution.py:423
  31.2 0.7 %copy.9 = bf16[4,128,128]{2,1,0:T(8,128)(2,1)} copy(bf16[4,128,128]{2,1,0:T(8,128)(2,1)S(1)} %triangles.1) | data formatting | bytes 262144

commit v4 on v3

--- a/solution.py
+++ b/solution.py
@@ -134,22 +134,22 @@
             push(src(spot ^ bits), dst, slot, me ^ bits)
             return carry
 
-        lax.fori_loop(1, group, one, 0)
-
-    def push_far(src, dst, slot):
+        lax.fori_loop(1, group, one, 0, unroll=True)
+
+    def push_far(src, dst, slot, turn_by=0):
         def one(step, carry):
-            bits = (group - step) ^ flip
+            bits = (group - step) ^ turn_by
             push(src(spot ^ bits), dst, slot, me ^ (group + bits))
             return carry
 
-        lax.fori_loop(1, group + 1, one, 0)
+        lax.fori_loop(1, group + 1, one, 0, unroll=True)
 
     def push_all(src, dst, slot):
         def one(step, carry):
             push(src, dst, slot, me ^ (devices - step))
             return carry
 
-        lax.fori_loop(1, devices, one, 0)
+        lax.fori_loop(1, devices, one, 0, unroll=True)
 
     def wait_all(buf, sem):
         pltpu.make_async_copy(buf, buf, sem).wait()
@@ -237,7 +237,7 @@
         normed = (normalize(new.astype(F32), 0) * lanes_of([normg_s[...]] * pairs)).astype(BF16)
         if part == 0:
             normed1_s[...] = normed
-        for side in range(2):
+        for side in (1, 0):
             panel = panels_of(1, normed, (1, 0), side) * scale_s[part]
             tile = jnp.concatenate(
                 [
@@ -247,9 +247,12 @@
                 axis=1,
             )
             c_send[part, :, side] = tile.astype(BF16)
+            if side == 1:
+                push_far(
+                    lambda at: c_send.at[part, at, 1], c_far.at[part, spot], 9 + part, flip
+                )
 
     def send_c(part):
-        push_far(lambda at: c_send.at[part, at, 1], c_far.at[part, spot], 9 + part)
         push_near(lambda at: c_send.at[part, at], c_near.at[part, spot], 7 + part)
         c_near[part, spot] = c_send[part, spot]
 
@@ -262,7 +265,7 @@
         near = c_near[part].astype(F32)
         lhs1_s[at, :] = near[:, 0].reshape(size, total)
         own1_s[at, :] = near[:, 1].reshape(size, total)
-        far1_s[at, :] = c_far[1 - part].astype(F32).reshape(size, total)
+        far1_s[pl.ds((1 - part) * size, size), :] = c_far[part].astype(F32).reshape(size, total)
 
     def incoming():
         count = HALVES * group * pairs
@@ -309,7 +312,7 @@
     with mark("sendA"):
         push_all(mask_send, mask_recv.at[me], 0)
         push_near(lambda at: a_send.at[at], a_near.at[spot], 1)
-        push_far(lambda at: a_send.at[at, 0], a_far.at[spot], 2)
+        push_far(lambda at: a_send.at[at, 0], a_far.at[spot], 2, flip)
         mask_recv[me] = mask_send[...]
         a_near[spot] = a_send[spot]
     with mark("idleA"):
@@ -368,17 +371,17 @@
     with mark("nat0"):
         z1_s[0] = z1t_s[0].astype(F32).T.astype(BF16)
         natural(0, normed1_s[...].astype(F32).T.astype(BF16))
-    with mark("back"):
-        wait_all(c_far.at[1], send_sems.at[10])
-        push(z1t_s.at[1], back_recv, 4, partner)
     with mark("waitC0"):
         wait_some(c_near.at[0], group - 1, recv_sems.at[7])
         wait_all(c_far.at[0], recv_sems.at[9])
+    with mark("back"):
+        push(z1t_s.at[1], back_recv, 4, partner)
+    with mark("unpack0"):
+        unpack1(0)
     with mark("waitC1"):
         wait_some(c_near.at[1], group - 1, recv_sems.at[8])
         wait_all(c_far.at[1], recv_sems.at[10])
     with mark("in"):
-        unpack1(0)
         unpack1(1)
         incoming()
     with mark("sendD"):
@@ -399,6 +402,8 @@
         for part in range(2):
             wait_some(b_recv.at[part], group - 1, send_sems.at[5 + part])
             wait_some(c_near.at[part], group - 1, send_sems.at[7 + part])
+        pass
+        wait_all(c_far.at[1], send_sems.at[10])
     with mark("waitD"):
         wait_some(d_recv, group - 1, recv_sems.at[11])
     with mark("finish1"):

time: 32 us -> 31.1 us (0.972)
  Pallas kernels: 31.2 us -> 30.3 us
    pallas_call x1, Pallas kernels: 31.2 us -> 30.3 us  [fused(): pl.pallas_call(functools.partial(fused_kernel, devices), out_shape=pltpu....]
where the time goes in v4:
time: 31.1 us; the launch traced here: 31 us
  Pallas kernels  30.3 us (97%)
  local copies, waits for them, and re-layouts  0.66 us (2%)
    pallas_call x1, Pallas kernels, fused(): pl.pallas_call(functools.partial(fused_kernel, devices), out_shape=pltpu....  30.3 us
    unnamed x1, local copies, waits for them, and re-layouts  0.66 us

profile of v4, /device:TPU:0, one launch (start us, length us, event | category | flops | bytes accessed | tf_op | source)
XLA Modules:
  0.0 31.0 jit_solution(13431332454701862288)
XLA Ops:
  0.0 30.3 %triangles.1 = bf16[4,128,128]{2,1,0:T(8,128)(2,1)S(1)} custom-call(bf16[4,128,128]{2,1,0:T(8,128)(2,1)} %pair_hbm.1, s32[4]{0:T(128)} %mask_hbm.1, f32[2,128]{1,0:T(2,128)} %norm_hbm.1, bf16[2,128,512]{2,1,0:T(8,128)(2,1)} %proj_hbm.1, bf16[2,128,128]{2,1,0:T(8,128)(2,1)} %gate_hbm.1, f32[2,128]{1,0:T(2,128)} %mix_hbm.1, bf16[2,128,128]{2,1,0:T(8,128)(2,1)} %outw_hbm.1), custom_call_target="tpu_custom_call" | custom-call | tf_op jit(solution)/shard_map/triangles/pallas_call | solution.py:428
  30.3 0.7 %copy.9 = bf16[4,128,128]{2,1,0:T(8,128)(2,1)} copy(bf16[4,128,128]{2,1,0:T(8,128)(2,1)S(1)} %triangles.1) | data formatting | bytes 262144

commit v5 on v4

--- a/solution.py
+++ b/solution.py
@@ -13,12 +13,20 @@
 BF16 = jnp.bfloat16
 MESH = pl.DeviceIdType.MESH
 HALVES = 2
+PAD = 8
 
 
 def normalize(values, axis):
     center = values - jnp.mean(values, axis=axis, keepdims=True)
     spread = jnp.mean(center * center, axis=axis, keepdims=True)
     return center * lax.rsqrt(spread + EPS)
+
+
+def normalize_down(values):
+    moved = values - values[:1]
+    center = jnp.mean(moved, axis=0, keepdims=True)
+    spread = jnp.mean(moved * moved, axis=0, keepdims=True) - center * center
+    return (moved - center) * lax.rsqrt(jnp.maximum(spread, 0.0) + EPS)
 
 
 def dot(a, b, dims):
@@ -85,6 +93,32 @@
     recv_sems,
     load_sems,
 ):
+    rows, total, chans = pair_ref.shape
+    hidden = mix_ref.shape[1]
+    group = devices // HALVES
+    own = hidden // group
+    cols = total // HALVES
+    spots = rows * cols
+    pairs = rows // 2
+    step = rows * own + PAD
+    me = lax.axis_index("dap")
+    half = me // group
+    spot = lax.rem(me, group)
+    partner = lax.rem(me + group, devices)
+    zone = me * 4 // devices
+    flip = jnp.where((zone == 0) | (zone == 3), group // 2, 0)
+    near_cols = pl.ds(pl.multiple_of(half * cols, cols), cols)
+    far_cols = pl.ds(pl.multiple_of((1 - half) * cols, cols), cols)
+
+    barrier = pltpu.get_barrier_semaphore()
+
+    def greet(step, carry):
+        peer = me ^ (devices - step)
+        pl.semaphore_signal(barrier, inc=1, device_id=(peer,), device_id_type=MESH)
+        return carry
+
+    lax.fori_loop(1, devices, greet, 0, unroll=True)
+
     sources = (pair_hbm, proj_hbm, mask_hbm, norm_hbm, gate_hbm, mix_hbm, outw_hbm)
     places = (pair_ref, proj_ref, mask_ref, norm_ref, gate_ref, mix_ref, outw_ref)
     loads = [
@@ -93,31 +127,6 @@
     ]
     for load in loads:
         load.start()
-    rows, total, chans = pair_ref.shape
-    hidden = mix_ref.shape[1]
-    group = devices // HALVES
-    own = hidden // group
-    cols = total // HALVES
-    spots = rows * cols
-    pairs = rows // 2
-    me = lax.axis_index("dap")
-    half = me // group
-    spot = lax.rem(me, group)
-    partner = lax.rem(me + group, devices)
-    zone = me * 4 // devices
-    flip = jnp.where((zone == 0) | (zone == 3), group // 2, 0)
-    near_cols = pl.ds(pl.multiple_of(half * cols, cols), cols)
-    far_cols = pl.ds(pl.multiple_of((1 - half) * cols, cols), cols)
-
-    barrier = pltpu.get_barrier_semaphore()
-
-    def greet(step, carry):
-        peer = me ^ (devices - step)
-        pl.semaphore_signal(barrier, inc=1, device_id=(peer,), device_id_type=MESH)
-        return carry
-
-    lax.fori_loop(1, devices, greet, 0)
-
     def push(src, dst, slot, peer):
         pltpu.make_async_remote_copy(
             src_ref=src,
@@ -199,13 +208,14 @@
         )
 
     def outgoing(part, panel):
-        left_s[part] = panel.astype(F32).reshape(group * rows * own, total)
+        for p in range(group):
+            left_s[part, p * step : p * step + rows * own, :] = panel[p].astype(F32)
         for c in range(own):
             left = jnp.concatenate(
                 [
                     lanes_of(
                         [
-                            left_s[part, pl.ds((2 * p + r) * own + c, group, stride=rows * own), :]
+                            left_s[part, pl.ds((2 * p + r) * own + c, group, stride=step), :]
                             for r in range(2)
                         ]
                     )
@@ -230,11 +240,16 @@
             [got[:, p * own : (p + 1) * own].reshape(hidden, total) for p in range(pairs)]
         )
         gain = mixg_s[0]
-        tri_normed = (normalize(tri, 0) * lanes_of([gain] * pairs)).astype(BF16)
-        out = dot(outw_s[...], tri_normed, (1, 0))
+        tri_normed = (normalize_down(tri) * lanes_of([gain] * pairs)).astype(BF16)
+        out = lanes_of(
+            [
+                dot(outw_s[...], tri_normed[:, p * total : (p + 1) * total], (1, 0))
+                for p in range(pairs)
+            ]
+        )
         new = (zt_s[part].astype(F32) + gate0_s[part] * out).astype(BF16)
         z1t_s[part] = new
-        normed = (normalize(new.astype(F32), 0) * lanes_of([normg_s[...]] * pairs)).astype(BF16)
+        normed = (normalize_down(new.astype(F32)) * lanes_of([normg_s[...]] * pairs)).astype(BF16)
         if part == 0:
             normed1_s[...] = normed
         for side in (1, 0):
@@ -272,9 +287,9 @@
         low = lane < cols
         for c in range(own):
             pick = pl.ds(c, count, stride=own)
-            left = lhs1_s[pick, :].astype(BF16)
+            left = lhs1_s[pick, :].astype(BF16).T
             right = lanes_of([own1_s[pick, :], far1_s[pick, :]]).astype(BF16)
-            prod = dot(left, right, (0, 0))
+            prod = dot(left, right, (1, 0))
             straight = jnp.where(low, prod[:cols, :total], prod[cols:, total:])
             crossed = jnp.where(low, prod[:cols, total:], prod[cols:, :total])
             tri = straight + pltpu.roll(crossed, cols, 1)
@@ -285,7 +300,7 @@
         got = d_recv[...].astype(F32)
         for r in range(rows):
             tri = got[:, r * own : (r + 1) * own].reshape(hidden, total)
-            tri_normed = (normalize(tri, 0) * mixg_s[1]).astype(BF16)
+            tri_normed = (normalize_down(tri) * mixg_s[1]).astype(BF16)
             out = dot(tri_normed, outw_ref[1], (0, 0))
             block = pl.ds(r * cols, cols)
             for part, place in enumerate((near_cols, far_cols)):
@@ -461,7 +476,7 @@
             pltpu.VMEM((2, chans, spots), F32),
             pltpu.VMEM((2, spots, chans), BF16),
             pltpu.VMEM((2, spots, chans), F32),
-            pltpu.VMEM((2, group * rows * own, total), F32),
+            pltpu.VMEM((2, group * (rows * own + PAD), total), F32),
             pltpu.VMEM((group * rows * own, total), F32),
             pltpu.VMEM((own, total, 2 * total), BF16),
             pltpu.VMEM((2, half_rows, total), F32),

time: 31.1 us -> 31 us (level)
  no operation moved by 1% of the time
where the time goes in v5:
time: 31 us; the launch traced here: 30.8 us
  Pallas kernels  30.2 us (97%)
  local copies, waits for them, and re-layouts  0.66 us (2%)
    pallas_call x1, Pallas kernels, fused(): pl.pallas_call(functools.partial(fused_kernel, devices), out_shape=pltpu....  30.2 us
    unnamed x1, local copies, waits for them, and re-layouts  0.66 us

profile of v5, /device:TPU:0, one launch (start us, length us, event | category | flops | bytes accessed | tf_op | source)
XLA Modules:
  0.0 30.8 jit_solution(2895119546015097913)
XLA Ops:
  0.0 30.2 %triangles.1 = bf16[4,128,128]{2,1,0:T(8,128)(2,1)S(1)} custom-call(bf16[4,128,128]{2,1,0:T(8,128)(2,1)} %pair_hbm.1, s32[4]{0:T(128)} %mask_hbm.1, f32[2,128]{1,0:T(2,128)} %norm_hbm.1, bf16[2,128,512]{2,1,0:T(8,128)(2,1)} %proj_hbm.1, bf16[2,128,128]{2,1,0:T(8,128)(2,1)} %gate_hbm.1, f32[2,128]{1,0:T(2,128)} %mix_hbm.1, bf16[2,128,128]{2,1,0:T(8,128)(2,1)} %outw_hbm.1), custom_call_target="tpu_custom_call" | custom-call | tf_op jit(solution)/shard_map/triangles/pallas_call | solution.py:443
  30.2 0.7 %copy.9 = bf16[4,128,128]{2,1,0:T(8,128)(2,1)} copy(bf16[4,128,128]{2,1,0:T(8,128)(2,1)S(1)} %triangles.1) | data formatting | bytes 262144

commit v6 on v5

--- a/solution.py
+++ b/solution.py
@@ -138,12 +138,11 @@
         ).start()
 
     def push_near(src, dst, slot):
-        def one(step, carry):
-            bits = group - step
-            push(src(spot ^ bits), dst, slot, me ^ bits)
-            return carry
-
-        lax.fori_loop(1, group, one, 0, unroll=True)
+        for step in range(group // 2):
+            high = group - 1 - step
+            for bits in (high, high ^ (group // 2) ^ 1):
+                if bits > 0:
+                    push(src(spot ^ bits), dst, slot, me ^ bits)
 
     def push_far(src, dst, slot, turn_by=0):
         def one(step, carry):

time: 31 us -> 30.9 us (level)
  no operation moved by 1% of the time
where the time goes in v6:
time: 30.9 us; the launch traced here: 30.8 us
  Pallas kernels  30.1 us (97%)
  local copies, waits for them, and re-layouts  0.66 us (2%)
    pallas_call x1, Pallas kernels, fused(): pl.pallas_call(functools.partial(fused_kernel, devices), out_shape=pltpu....  30.1 us
    unnamed x1, local copies, waits for them, and re-layouts  0.66 us

profile of v6, /device:TPU:0, one launch (start us, length us, event | category | flops | bytes accessed | tf_op | source)
XLA Modules:
  0.0 30.8 jit_solution(12654227833148196852)
XLA Ops:
  0.0 30.1 %triangles.1 = bf16[4,128,128]{2,1,0:T(8,128)(2,1)S(1)} custom-call(bf16[4,128,128]{2,1,0:T(8,128)(2,1)} %pair_hbm.1, s32[4]{0:T(128)} %mask_hbm.1, f32[2,128]{1,0:T(2,128)} %norm_hbm.1, bf16[2,128,512]{2,1,0:T(8,128)(2,1)} %proj_hbm.1, bf16[2,128,128]{2,1,0:T(8,128)(2,1)} %gate_hbm.1, f32[2,128]{1,0:T(2,128)} %mix_hbm.1, bf16[2,128,128]{2,1,0:T(8,128)(2,1)} %outw_hbm.1), custom_call_target="tpu_custom_call" | custom-call | tf_op jit(solution)/shard_map/triangles/pallas_call | solution.py:442
  30.1 0.7 %copy.9 = bf16[4,128,128]{2,1,0:T(8,128)(2,1)} copy(bf16[4,128,128]{2,1,0:T(8,128)(2,1)S(1)} %triangles.1) | data formatting | bytes 262144

commit v7 on v6

--- a/solution.py
+++ b/solution.py
@@ -309,7 +309,7 @@
 
     lane = lax.broadcasted_iota(jnp.int32, (1, total), 1)
     with mark("load"):
-        for load in loads:
+        for load in loads[:4]:
             load.wait()
     with mark("panels0"):
         mask_row = jnp.zeros((1, total), F32)
@@ -330,6 +330,8 @@
         mask_recv[me] = mask_send[...]
         a_near[spot] = a_send[spot]
     with mark("idleA"):
+        for load in loads[4:]:
+            load.wait()
         gatew_s[...] = turn(gate_ref[0])
         outw_s[...] = turn(outw_ref[0])
         weight_s[1] = turn(proj_ref[1])

time: 30.9 us -> 30.9 us (level)
  no operation moved by 1% of the time
where the time goes in v7:
time: 30.9 us; the launch traced here: 30.8 us
  Pallas kernels  30.1 us (97%)
  local copies, waits for them, and re-layouts  0.66 us (2%)
    pallas_call x1, Pallas kernels, fused(): pl.pallas_call(functools.partial(fused_kernel, devices), out_shape=pltpu....  30.1 us
    unnamed x1, local copies, waits for them, and re-layouts  0.66 us

profile of v7, /device:TPU:0, one launch (start us, length us, event | category | flops | bytes accessed | tf_op | source)
XLA Modules:
  0.0 30.8 jit_solution(7996246812184051730)
XLA Ops:
  0.0 30.1 %triangles.1 = bf16[4,128,128]{2,1,0:T(8,128)(2,1)S(1)} custom-call(bf16[4,128,128]{2,1,0:T(8,128)(2,1)} %pair_hbm.1, s32[4]{0:T(128)} %mask_hbm.1, f32[2,128]{1,0:T(2,128)} %norm_hbm.1, bf16[2,128,512]{2,1,0:T(8,128)(2,1)} %proj_hbm.1, bf16[2,128,128]{2,1,0:T(8,128)(2,1)} %gate_hbm.1, f32[2,128]{1,0:T(2,128)} %mix_hbm.1, bf16[2,128,128]{2,1,0:T(8,128)(2,1)} %outw_hbm.1), custom_call_target="tpu_custom_call" | custom-call | tf_op jit(solution)/shard_map/triangles/pallas_call | solution.py:444
  30.1 0.7 %copy.9 = bf16[4,128,128]{2,1,0:T(8,128)(2,1)} copy(bf16[4,128,128]{2,1,0:T(8,128)(2,1)S(1)} %triangles.1) | data formatting | bytes 262144
